TPU v7x, 8 devices: a whole 2x2x1 slice. The times are simulated.
8 devices in a mesh: rep: 1 (over z), r: 2 (over y), s: 4 (over x, core).
Axes of the slice: x: 2, y: 2, z: 1, core: 2. Of those that a mesh axis runs over, the one named last changes fastest.
Arguments:
- x: bfloat16 [8, 4096, 1024], P(('rep', 'r', 's'))
- dy: bfloat16 [8, 4096, 1024], P(('rep', 'r', 's'))
- w_gate: bfloat16 [2, 1024, 2560], P(None, 's')
- w_up: bfloat16 [2, 1024, 2560], P(None, 's')
- w_down: bfloat16 [2, 2560, 1024], P(None, 's')
- m_w_gate: float32 [2, 1024, 2560], P(None, 's')
- m_w_up: float32 [2, 1024, 2560], P(None, 's')
- m_w_down: float32 [2, 2560, 1024], P(None, 's')
- v_w_gate: float32 [2, 1024, 2560], P(None, 's')
- v_w_up: float32 [2, 1024, 2560], P(None, 's')
- v_w_down: float32 [2, 2560, 1024], P(None, 's')
Outputs:
- output 1: bfloat16 [2, 1024, 2560], P('rep', 's')
- output 2: bfloat16 [2, 1024, 2560], P('rep', 's')
- output 3: bfloat16 [2, 2560, 1024], P('rep', 's')
- output 4: float32 [2, 1024, 2560], P('rep', 's')
- output 5: float32 [2, 1024, 2560], P('rep', 's')
- output 6: float32 [2, 2560, 1024], P('rep', 's')
- output 7: float32 [2, 1024, 2560], P('rep', 's')
- output 8: float32 [2, 1024, 2560], P('rep', 's')
- output 9: float32 [2, 2560, 1024], P('rep', 's')
All inputs are finite; a program needn't handle non-finite values.
Results may differ from a plain program's by a relative error of at most 0.022.
Values are sent between devices in bfloat16 or wider.
A program may use at most 2 GiB of HBM per device.

v0:
```python
import jax
import jax.numpy as jnp
from jax import lax
from jax.sharding import PartitionSpec as P

NAMES = ("w_gate", "w_up", "w_down")


def matmul(a, w):
    return jnp.dot(a, w, preferred_element_type=jnp.float32).astype(jnp.bfloat16)


def normed(h):
    wide = h.astype(jnp.float32)
    scale = lax.rsqrt(jnp.mean(wide**2, -1, keepdims=True) + 1e-6)
    return (wide * scale).astype(jnp.bfloat16)


def layer(h, w):
    a = normed(h)
    gate = jnp.dot(a, w["w_gate"], preferred_element_type=jnp.float32)
    up = jnp.dot(a, w["w_up"], preferred_element_type=jnp.float32)
    return h + matmul((jax.nn.silu(gate) * up).astype(jnp.bfloat16), w["w_down"])


def adamw(w, m, v, g):
    m = 0.9 * m + 0.1 * g
    v = 0.95 * v + 0.05 * g * g
    step = m * lax.rsqrt(v + 1e-8) + 0.1 * w
    return (w - 0.02 * step).astype(jnp.bfloat16), m, v


def clipped(gradients, sum_of_squares, count):
    factor = jnp.minimum(1.0, 0.5 * lax.rsqrt(sum_of_squares / count + 1e-30))
    return [g * factor for g in gradients]


def solution(mesh):
    def fetched(weights, number):
        return {name: lax.all_gather(w[number], "s", axis=0, tiled=True) for name, w in zip(NAMES, weights, strict=True)}

    def summed(term):
        return lax.psum(lax.psum_scatter(term, "s", scatter_dimension=0, tiled=True), "r")

    def step(x, dy, *arrays):
        weights, m, v = (arrays[i : i + 3] for i in (0, 3, 6))
        layers = weights[0].shape[0]
        h, kept = x[0], []
        for number in range(layers):
            kept.append(h)
            h = layer(h, fetched(weights, number))
        by_h, mine = dy[0], [None] * layers
        for number in reversed(range(layers)):
            _, back = jax.vjp(lambda w, h: layer(h, w), fetched(weights, number), kept[number])
            by_w, by_h = back(by_h)
            mine[number] = [summed(by_w[name]) for name in NAMES]
        gradients = [jnp.stack([mine[number][i] for number in range(layers)]).astype(jnp.float32) for i in range(3)]
        squares = lax.psum(sum(jnp.sum(g * g) for g in gradients), "s")
        gradients = clipped(gradients, squares, lax.psum(1, "s") * sum(g.size for g in gradients))
        new = [adamw(w.astype(jnp.float32), m, v, g) for w, m, v, g in zip(weights, m, v, gradients, strict=True)]
        return tuple(one[which] for which in range(3) for one in new)

    states, cut = P(("rep", "r", "s"), None, None), P(None, "s", None)
    return jax.shard_map(
        step,
        mesh=mesh,
        in_specs=(states, states) + (cut,) * 9,
        out_specs=(P("rep", "s", None),) * 9,
        check_vma=False,
    )
```

profile of v0, /device:TPU:0, one launch (start us, length us, event | category | flops | bytes accessed | tf_op | source)
XLA Modules:
  0.0 944.7 jit_solution(4606049880380430475)
XLA Ops:
  17.8 11.2 %copy.20 = bf16[1,4096,1024]{1,2,0:T(8,128)(2,1)} copy(bf16[1,4096,1024]{2,1,0:T(8,128)(2,1)} %param.11) | data formatting | bytes 16777216 | tf_op args[0]
  29.1 5.1 fusion.15
  34.2 11.4 %copy.21 = bf16[1,4096,1024]{1,2,0:T(8,128)(2,1)} copy(bf16[1,4096,1024]{2,1,0:T(8,128)(2,1)} %param.12) | data formatting | bytes 16777216 | tf_op args[1]
  45.6 5.7 all-gather.13.cloned.1.call-done
  51.3 29.7 %fusion.47 = f32[4096,2560]{1,0:T(8,128)} fusion(bf16[1,4096,1024]{1,2,0:T(8,128)(2,1)} %copy.20, f32[4096]{0:T(1024)S(1)} %add_rsqrt_fusion, bf16[1,1024,2560]{2,1,0:T(8,128)(2,1)} %all-gather.13.cloned.1.call-done), kind=kOutput, calls=%fused_computation.72 | convolution fusion | flops 21487419392 | bytes 55590912 | tf_op jit(solution)/shard_map/dot_general | solution.py:21
  81.0 10.0 %all-gather.15.cloned.1.call-done = bf16[1,1024,2560]{2,1,0:T(8,128)(2,1)} async-done(((bf16[1,256,2560]{2,1,0:T(8,128)(2,1)}), bf16[1,1024,2560]{2,1,0:T(8,128)(2,1)}) %all-gather.15.cloned.1.call-update) | async-done | bytes 5242896 | tf_op jit(solution)/shard_map/all_gather | solution.py:40
  91.0 50.2 %multiply_convert_fusion.1 = (bf16[4096,2560]{1,0:T(8,128)(2,1)}, f32[4096,2560]{1,0:T(8,128)}) fusion(f32[4096,2560]{1,0:T(8,128)} %fusion.47, bf16[1,1024,2560]{2,1,0:T(8,128)(2,1)} %all-gather.15.cloned.1.call-done, bf16[1,4096,1024]{1,2,0:T(8,128)(2,1)} %copy.20, f32[4096]{0:T(1024)S(1)} %add_rsqrt_fusion), kind=kOutput, calls=%fused_computation.17 | convolution fusion | flops 21550333952 | bytes 118505472 | tf_op jit(solution)/shard_map/dot_general | solution.py:22
  141.3 29.8 %fusion.19 = (f32[4096]{0:T(1024)S(1)}, bf16[4096,1024]{0,1:T(8,128)(2,1)}) fusion(bf16[4096,2560]{1,0:T(8,128)(2,1)} %get-tuple-element.30, bf16[1,2560,1024]{2,1,0:T(8,128)(2,1)} %all-gather.17.cloned.1.call-done, bf16[1,4096,1024]{1,2,0:T(8,128)(2,1)} %copy.20), kind=kOutput, calls=%fused_computation.37 | convolution fusion | flops 21495803904 | bytes 43008000 | tf_op jit(solution)/shard_map/dot_general | solution.py:10
  171.7 29.1 %convolution_convert_fusion.1 = bf16[4096,2560]{1,0:T(8,128)(2,1)} fusion(bf16[1,4096,1024]{2,1,0:T(8,128)(2,1)} %param.12, bf16[1,2560,1024]{2,1,0:T(8,128)(2,1)} %all-gather.21.cloned.1.call-done), kind=kOutput, calls=%fused_computation.27 | convolution fusion | flops 21485322240 | bytes 34603008 | tf_op jit(solution)/shard_map/transpose(jvp())/dot_general | solution.py:10
  200.8 9.0 all-gather.23.cloned.1.call-done
  209.8 29.7 %fusion.39 = f32[4096,2560]{1,0:T(8,128)} fusion(bf16[4096,1024]{0,1:T(8,128)(2,1)} %get-tuple-element.33, f32[4096]{0:T(1024)S(1)} %fusion.77, bf16[1,1024,2560]{2,1,0:T(8,128)(2,1)} %all-gather.23.cloned.1.call-done), kind=kOutput, calls=%fused_computation.69 | convolution fusion | flops 21487419392 | bytes 55590912 | tf_op jit(solution)/shard_map/jvp()/dot_general | solution.py:22
  239.5 9.8 %all-gather.19.cloned.1.call-done = bf16[1,1024,2560]{2,1,0:T(8,128)(2,1)} async-done(((bf16[1,256,2560]{2,1,0:T(8,128)(2,1)}), bf16[1,1024,2560]{2,1,0:T(8,128)(2,1)}) %all-gather.19.cloned.1.call-update) | async-done | bytes 5242896 | tf_op jit(solution)/shard_map/all_gather | solution.py:40
  249.3 58.5 %fusion.2 = (bf16[4096,2560]{1,0:T(8,128)(2,1)}, f32[4096,2560]{1,0:T(8,128)}) fusion(f32[4096,2560]{1,0:T(8,128)} %fusion.39, bf16[4096,2560]{1,0:T(8,128)(2,1)} %convolution_convert_fusion.1, bf16[1,1024,2560]{2,1,0:T(8,128)(2,1)} %all-gather.19.cloned.1.call-done, bf16[4096,1024]{0,1:T(8,128)(2,1)} %get-tuple-element.33, f32[4096]{0:T(1024)S(1)} %fusion.77), kind=kOutput, calls=%fused_computation.8 | convolution fusion | flops 21613248512 | bytes 139476992 | tf_op jit(solution)/shard_map/jvp()/dot_general | solution.py:21
  307.9 26.4 %fusion.70 = bf16[4096,1024]{0,1:T(8,128)(2,1)} fusion(bf16[4096,2560]{1,0:T(8,128)(2,1)} %get-tuple-element.34, bf16[1,1024,2560]{2,1,0:T(8,128)(2,1)S(1)} %copy-done.15), kind=kOutput, calls=%fused_computation.94 | convolution fusion | flops 21474836480 | bytes 34603008 | tf_op jit(solution)/shard_map/transpose(jvp())/dot_general | solution.py:21
  334.3 38.8 %fusion.21 = (f32[4096]{0:T(1024)S(1)}, bf16[4096,1024]{0,1:T(8,128)(2,1)}) fusion(bf16[4096,1024]{0,1:T(8,128)(2,1)} %get-tuple-element.33, bf16[4096,1024]{0,1:T(8,128)(2,1)} %fusion.70, bf16[1,1024,2560]{2,1,0:T(8,128)(2,1)} %all-gather.23.cloned.1.call-done, bf16[4096,2560]{1,0:T(8,128)(2,1)} %convolution_convert_fusion.1, ...), kind=kOutput, calls=%fused_computation.39 | convolution fusion | flops 21562912768 | bytes 93339648 | tf_op jit(solution)/shard_map/transpose(jvp())/dot_general | solution.py:22
  373.1 10.9 %fusion.22 = bf16[4096,1024]{0,1:T(8,128)(2,1)S(1)} fusion(bf16[4096,1024]{0,1:T(8,128)(2,1)} %get-tuple-element.33, bf16[4096,1024]{0,1:T(8,128)(2,1)} %get-tuple-element.37, bf16[1,4096,1024]{1,2,0:T(8,128)(2,1)} %copy.21, f32[4096]{0:T(1024)S(1)} %multiply_multiply_fusion.3, f32[4096]{0:T(1024)S(1)} %fusion.77), kind=kLoop, calls=%fused_computation.40 | loop fusion | flops 29360128 | bytes 33587200 | tf_op jit(solution)/shard_map/transpose(jvp())/add_any | solution.py:14
  387.3 26.5 %convolution_convert_fusion.2 = bf16[2560,1024]{1,0:T(8,128)(2,1)} fusion(bf16[4096,2560]{1,0:T(8,128)(2,1)} %get-tuple-element.30, bf16[4096,1024]{0,1:T(8,128)(2,1)S(1)} %fusion.22), kind=kOutput, calls=%fused_computation.67 | convolution fusion | flops 21477457920 | bytes 34603008 | tf_op jit(solution)/shard_map/transpose(jvp())/dot_general | solution.py:10
  413.8 36.2 %fusion.32 = bf16[2560,1024]{1,0:T(8,128)(2,1)} fusion(bf16[1,4096,1024]{2,1,0:T(8,128)(2,1)} %param.12, f32[4096,2560]{1,0:T(8,128)} %fusion.39, f32[4096,2560]{1,0:T(8,128)} %get-tuple-element.35), kind=kOutput, calls=%fused_computation.64 | convolution fusion | flops 21540372480 | bytes 97517568 | tf_op jit(solution)/shard_map/transpose(jvp())/dot_general | solution.py:10
  450.1 28.2 %convolution_convert_fusion = bf16[4096,2560]{1,0:T(8,128)(2,1)} fusion(bf16[4096,1024]{0,1:T(8,128)(2,1)} %copy-done.4, bf16[1,2560,1024]{2,1,0:T(8,128)(2,1)} %all-gather.17.cloned.1.call-done), kind=kOutput, calls=%fused_computation.26 | convolution fusion | flops 21485322240 | bytes 34603008 | tf_op jit(solution)/shard_map/transpose(jvp())/dot_general | solution.py:10
  478.3 37.1 %fusion.36 = bf16[1024,2560]{1,0:T(8,128)(2,1)} fusion(bf16[4096,2560]{1,0:T(8,128)(2,1)} %convolution_convert_fusion, f32[4096,2560]{1,0:T(8,128)} %fusion.47, bf16[1,4096,1024]{1,2,0:T(8,128)(2,1)} %copy.20, f32[4096]{0:T(1024)S(1)} %copy-done.14), kind=kOutput, calls=%fused_computation.66 | convolution fusion | flops 21552955392 | bytes 76562432 | tf_op jit(solution)/shard_map/transpose(jvp())/dot_general | solution.py:22
  515.5 37.4 %fusion.35 = bf16[1024,2560]{1,0:T(8,128)(2,1)} fusion(bf16[4096,2560]{1,0:T(8,128)(2,1)} %convolution_convert_fusion.1, bf16[4096,1024]{0,1:T(8,128)(2,1)} %get-tuple-element.33, f32[4096]{0:T(1024)S(1)} %copy-done.10, f32[4096,2560]{1,0:T(8,128)} %get-tuple-element.35), kind=kOutput, calls=%fused_computation.65 | convolution fusion | flops 21552955392 | bytes 76562432 | tf_op jit(solution)/shard_map/transpose(jvp())/dot_general | solution.py:22
  553.0 44.3 %fusion.29 = bf16[1024,2560]{1,0:T(8,128)(2,1)} fusion(f32[4096,2560]{1,0:T(8,128)} %fusion.47, f32[4096,2560]{1,0:T(8,128)} %get-tuple-element.31, bf16[4096,2560]{1,0:T(8,128)(2,1)} %convolution_convert_fusion, bf16[1,4096,1024]{1,2,0:T(8,128)(2,1)} %copy.20, f32[4096]{0:T(1024)S(1)} %copy-done.14), kind=kOutput, calls=%fused_computation.63 | convolution fusion | flops 21605384192 | bytes 118505472 | tf_op jit(solution)/shard_map/transpose(jvp())/dot_general | solution.py:21
  597.4 28.6 %convolution_convert_fusion.3 = bf16[1024,2560]{1,0:T(8,128)(2,1)} fusion(bf16[4096,2560]{1,0:T(8,128)(2,1)} %get-tuple-element.34, bf16[4096,1024]{0,1:T(8,128)(2,1)} %get-tuple-element.33, f32[4096]{0:T(1024)S(1)} %copy-done.10), kind=kOutput, calls=%fused_computation.68 | convolution fusion | flops 21487419392 | bytes 34619392 | tf_op jit(solution)/shard_map/transpose(jvp())/dot_general | solution.py:21
  626.1 29.9 %reduce-scatter.7.cloned.1.call-done = bf16[256,2560]{1,0:T(8,128)(2,1)} async-done(((bf16[1024,2560]{1,0:T(8,128)(2,1)}), bf16[256,2560]{1,0:T(8,128)(2,1)}) %reduce-scatter.7.cloned.1.call-update) | async-done | bytes 1310736 | tf_op jit(solution)/shard_map/reduce_scatter | solution.py:43
  656.1 47.8 %reduce-scatter.9.cloned.1.call-done = bf16[256,2560]{1,0:T(8,128)(2,1)} async-done(((bf16[1024,2560]{1,0:T(8,128)(2,1)}), bf16[256,2560]{1,0:T(8,128)(2,1)}) %reduce-scatter.9.cloned.1.call-update) | async-done | bytes 1310736 | tf_op jit(solution)/shard_map/reduce_scatter | solution.py:43
  703.9 184.4 %all-reduce.3.cloned.1.call-done = (bf16[1,256,2560]{2,1,0:T(8,128)(2,1)}, bf16[1,256,2560]{2,1,0:T(8,128)(2,1)}, bf16[1,256,2560]{2,1,0:T(8,128)(2,1)}, bf16[1,...) async-done(((bf16[1,256,2560]{2,1,0:T(8,128)(2,1)}, bf16[1,256,2560]{2,1,0:T(8,128)(2,1)}, bf16[1,256,2560]{2,1,0:T(8,128)(2,1)}, ...) | async-done | bytes 7864336 | tf_op jit(solution)/shard_map/psum | solution.py:43
  888.2 3.7 fusion.57
  891.9 3.7 fusion.56
  895.5 3.7 fusion.55
  901.2 6.8 psum.55
  908.7 11.1 %fusion.63 = (bf16[2,640,1024]{2,1,0:T(8,128)(2,1)}, f32[2,640,1024]{2,1,0:T(8,128)}, f32[2,640,1024]{2,1,0:T(8,128)}) fusion(bf16[2,640,1024]{2,1,0:T(8,128)(2,1)S(1)} %copy-done.3, f32[]{:T(128)S(6)} %min_shard_map.3, bf16[1,640,1024]{2,1,0:T(8,128)(2,1)} %get-tuple-element.13, bf16[1,640,1024]{2,1,0:T(8,128)(2,1)} %get-tuple-element.14, ...), kind=kLoop, calls=%fused_computation.87 | loop fusion | flops 26214400 | bytes 28835844 | tf_op jit(solution)/shard_map/convert_element_type | solution.py:30
  921.0 16.8 %fusion.54 = (bf16[2,256,2560]{2,1,0:T(8,128)(2,1)}, f32[2,256,2560]{2,1,0:T(8,128)}, f32[2,256,2560]{2,1,0:T(8,128)}, bf16[2,256,2560]{2,1,0:T(8,128)(2,1)}, f3...) fusion(bf16[2,256,2560]{2,1,0:T(8,128)(2,1)S(1)} %copy-done, f32[]{:T(128)S(6)} %min_shard_map.3, ...), kind=kLoop, calls=%fused_computation.78 | loop fusion | flops 52428800 | bytes 57671684 | tf_op jit(solution)/shard_map/convert_element_type | solution.py:30
  (70 shorter events, 16.1 us)
Async XLA Ops:
  7.2 7.1 copy-start.2
  7.2 44.1 %all-gather.13.cloned.1.call-start = ((), (), s32[]{:S(2)}) async-start(), calls=%async_computation.12 | async-start | bytes 6553600 | tf_op jit(solution)/shard_map/all_gather | solution.py:40
  10.8 80.2 %all-gather.15.cloned.1.call-start = ((), (), s32[]{:S(2)}) async-start(), calls=%async_computation.13 | async-start | bytes 6553600 | tf_op jit(solution)/shard_map/all_gather | solution.py:40
  14.2 127.0 %all-gather.17.cloned.1.call-start = ((), (), s32[]{:S(2)}) async-start(), calls=%async_computation.14 | async-start | bytes 6553600 | tf_op jit(solution)/shard_map/all_gather | solution.py:40
  16.0 155.7 %all-gather.21.cloned.1.call-start = ((), (), s32[]{:S(2)}) async-start(), calls=%async_computation.16 | async-start | bytes 6553600 | tf_op jit(solution)/shard_map/all_gather | solution.py:40
  16.6 193.2 %all-gather.23.cloned.1.call-start = ((), (), s32[]{:S(2)}) async-start(), calls=%async_computation.17 | async-start | bytes 6553600 | tf_op jit(solution)/shard_map/all_gather | solution.py:40
  17.2 232.1 %all-gather.19.cloned.1.call-start = ((), (), s32[]{:S(2)}) async-start(), calls=%async_computation.15 | async-start | bytes 6553600 | tf_op jit(solution)/shard_map/all_gather | solution.py:40
  17.8 608.2 %reduce-scatter.15.cloned.1.call-start = ((), (), s32[]{:S(2)}) async-start(), calls=%async_computation.10 | async-start | bytes 6553600 | tf_op jit(solution)/shard_map/reduce_scatter | solution.py:43
  34.2 56.9 %copy-start.13 = (f32[4096]{0:T(1024)}, f32[4096]{0:T(1024)S(1)}, u32[]{:S(2)}) copy-start(f32[4096]{0:T(1024)S(1)} %add_rsqrt_fusion) | copy-start | bytes 49156
  171.0 0.6 copy-start.11
  171.7 201.4 %copy-start.9 = (f32[4096]{0:T(1024)}, f32[4096]{0:T(1024)S(1)}, u32[]{:S(2)}) copy-start(f32[4096]{0:T(1024)S(1)} %fusion.77) | copy-start | bytes 49156
  249.3 58.6 %copy-start.15 = (bf16[1,1024,2560]{2,1,0:T(8,128)(2,1)S(1)}, bf16[1,1024,2560]{2,1,0:T(8,128)(2,1)}, u32[]{:S(2)}) copy-start(bf16[1,1024,2560]{2,1,0:T(8,128)(2,1)} %all-gather.19.cloned.1.call-done) | copy-start | bytes 15728644
  334.3 38.8 %copy-start.12 = (f32[4096]{0:T(1024)S(1)}, f32[4096]{0:T(1024)}, u32[]{:S(2)}) copy-start(f32[4096]{0:T(1024)} %copy-done.11) | copy-start | bytes 49156
  384.0 3.2 copy-start.4
  413.7 212.3 %reduce-scatter.17.cloned.1.call-start = ((), (), s32[]{:S(2)}) async-start(), calls=%async_computation.11 | async-start | bytes 6553600 | tf_op jit(solution)/shard_map/reduce_scatter | solution.py:43
  450.0 28.2 %copy-start.14 = (f32[4096]{0:T(1024)S(1)}, f32[4096]{0:T(1024)}, u32[]{:S(2)}) copy-start(f32[4096]{0:T(1024)} %copy-done.13) | copy-start | bytes 49156
  450.0 176.1 %reduce-scatter.11.cloned.1.call-start = ((), (), s32[]{:S(2)}) async-start(), calls=%async_computation.8 | async-start | bytes 6553600 | tf_op jit(solution)/shard_map/reduce_scatter | solution.py:43
  478.3 37.2 %copy-start.10 = (f32[4096]{0:T(1024)S(1)}, f32[4096]{0:T(1024)}, u32[]{:S(2)}) copy-start(f32[4096]{0:T(1024)} %copy-done.9) | copy-start | bytes 49156
  515.4 110.7 %reduce-scatter.13.cloned.1.call-start = ((), (), s32[]{:S(2)}) async-start(), calls=%async_computation.9 | async-start | bytes 6553600 | tf_op jit(solution)/shard_map/reduce_scatter | solution.py:43
  552.9 103.1 %reduce-scatter.7.cloned.1.call-start = ((), (), s32[]{:S(2)}) async-start(), calls=%async_computation.6 | async-start | bytes 6553600 | tf_op jit(solution)/shard_map/reduce_scatter | solution.py:43
  597.3 106.5 %reduce-scatter.9.cloned.1.call-start = ((), (), s32[]{:S(2)}) async-start(), calls=%async_computation.7 | async-start | bytes 6553600 | tf_op jit(solution)/shard_map/reduce_scatter | solution.py:43
  625.9 282.7 %copy-start.3 = (bf16[2,640,1024]{2,1,0:T(8,128)(2,1)S(1)}, bf16[2,640,1024]{2,1,0:T(8,128)(2,1)}, u32[]{:S(2)}) copy-start(bf16[2,640,1024]{2,1,0:T(8,128)(2,1)} %param.15) | copy-start | bytes 7864324
  626.0 262.3 %all-reduce.3.cloned.1.call-start = ((), (), s32[]{:S(2)}) async-start(), calls=%async_computation.18 | async-start | bytes 15728640 | tf_op jit(solution)/shard_map/psum | solution.py:43
  908.7 11.2 %copy-start = (bf16[2,256,2560]{2,1,0:T(8,128)(2,1)S(1)}, bf16[2,256,2560]{2,1,0:T(8,128)(2,1)}, u32[]{:S(2)}) copy-start(bf16[2,256,2560]{2,1,0:T(8,128)(2,1)} %param.13) | copy-start | bytes 7864324
  908.7 11.1 %copy-start.1 = (bf16[2,256,2560]{2,1,0:T(8,128)(2,1)S(1)}, bf16[2,256,2560]{2,1,0:T(8,128)(2,1)}, u32[]{:S(2)}) copy-start(bf16[2,256,2560]{2,1,0:T(8,128)(2,1)} %param.14) | copy-start | bytes 7864324
  908.7 11.1 %copy-start.5 = (bf16[1,256,2560]{2,1,0:T(8,128)(2,1)S(1)}, bf16[1,256,2560]{2,1,0:T(8,128)(2,1)}, u32[]{:S(2)}) copy-start(bf16[1,256,2560]{2,1,0:T(8,128)(2,1)} %get-tuple-element.9) | copy-start | bytes 3932164
  908.7 11.1 %copy-start.6 = (bf16[1,256,2560]{2,1,0:T(8,128)(2,1)S(1)}, bf16[1,256,2560]{2,1,0:T(8,128)(2,1)}, u32[]{:S(2)}) copy-start(bf16[1,256,2560]{2,1,0:T(8,128)(2,1)} %get-tuple-element.10) | copy-start | bytes 3932164
  908.7 11.5 %copy-start.7 = (bf16[1,256,2560]{2,1,0:T(8,128)(2,1)S(1)}, bf16[1,256,2560]{2,1,0:T(8,128)(2,1)}, u32[]{:S(2)}) copy-start(bf16[1,256,2560]{2,1,0:T(8,128)(2,1)} %get-tuple-element.11) | copy-start | bytes 3932164
  908.7 12.3 %copy-start.8 = (bf16[1,256,2560]{2,1,0:T(8,128)(2,1)S(1)}, bf16[1,256,2560]{2,1,0:T(8,128)(2,1)}, u32[]{:S(2)}) copy-start(bf16[1,256,2560]{2,1,0:T(8,128)(2,1)} %get-tuple-element.12) | copy-start | bytes 3932164
Sparse Core Ops, SparseCore 0:
  10.9 40.3 all-gather.12
  53.4 37.5 all-gather.14
  93.1 37.5 all-gather.16
  132.7 37.5 all-gather.20
  172.2 37.5 all-gather.22
  211.7 37.5 all-gather.18
  413.9 44.8 reduce-scatter.14
  461.8 44.8 reduce-scatter.16
  515.5 44.8 reduce-scatter.10
  563.3 44.8 reduce-scatter.12
  611.2 44.8 reduce-scatter.6
  659.0 44.8 reduce-scatter.8
  706.8 181.3 all-reduce.2
where the time goes:
time: 952 us; the launch traced here: 945 us
  matrix products  531 us (56%)
  waiting for transfers between devices  298 us (31%)
  other arithmetic  54.9 us (6%)
  local copies, waits for them, and re-layouts  36.4 us (4%)
  between operations  17.2 us (2%)
    dot_general x5, matrix products, layer(): up = jnp.dot(a, w['w_up'], preferred_element_type=jnp.float32)  193 us
    dot_general x5, matrix products, layer(): gate = jnp.dot(a, w['w_gate'], preferred_element_type=jnp.float32)  187 us
    psum x1, waiting for transfers between devices, summed(): lax.psum(lax.psum_scatter(term, 's', scatter_dimension=0, tiled=True), 'r')  184 us
    dot_general x5, matrix products, matmul(): jnp.dot(a, w, preferred_element_type=jnp.float32).astype(jnp.bfloat16)  150 us
    reduce_scatter x6, waiting for transfers between devices, summed(): lax.psum_scatter(term, 's', scatter_dimension=0, tiled=True)  77.8 us
    all_gather x6, waiting for transfers between devices, fetched(): lax.all_gather(w[number], 's', axis=0, tiled=True)  34.5 us
    convert_element_type x2, other arithmetic, adamw(): return ((w - 0.02 * step).astype(jnp.bfloat16), m, v)  27.9 us
    unnamed x34, local copies, waits for them, and re-layouts  27.7 us
  transfers between devices with their start and end apart: 13, of which 7 were waited for; matrix products, arithmetic and copies ran while one was open for 44% of the time, Pallas kernels for 0%

commit v1 on v0

v1 whole, which is shorter than its diff:
```python
import functools

import jax
import jax.numpy as jnp
from jax import lax
from jax.experimental import pallas as pl
from jax.experimental.pallas import tpu as pltpu
from jax.sharding import PartitionSpec as P

NAMES = ("w_gate", "w_up", "w_down")
TOK, D, FF = 4096, 1024, 2560
NC, CH = 5, 512
bf16, f32 = jnp.bfloat16, jnp.float32
PARAMS = pltpu.CompilerParams(vmem_limit_bytes=62 * 1024 * 1024)


def dot(a, b):
    return jnp.dot(a, b, preferred_element_type=f32)


def dot_nt(a, b):
    return lax.dot_general(a, b, (((1,), (1,)), ((), ())), preferred_element_type=f32)


def dot_tn(a, b):
    return lax.dot_general(a, b, (((0,), (0,)), ((), ())), preferred_element_type=f32)


def cost(products, width, nbytes):
    return pl.CostEstimate(flops=products * 2 * TOK * D * width, bytes_accessed=nbytes, transcendentals=0)


def scale_of(wide):
    return lax.rsqrt(jnp.mean(wide * wide, -1, keepdims=True) + 1e-6)


def sigmoid(g):
    return 0.5 * jnp.tanh(0.5 * g) + 0.5


def once(shape):
    return pl.BlockSpec(shape, lambda *_: (0,) * len(shape), pipeline_mode=pl.Buffered(1))


def forward_up(x, wg, wu, TM=256):
    def body(x_ref, wg_ref, wu_ref, a_ref, g_ref, u_ref, hid_ref):
        wide = x_ref[...].astype(f32)
        a = (wide * scale_of(wide)).astype(bf16)
        a_ref[...] = a
        for n in range(NC):
            c = slice(n * CH, (n + 1) * CH)
            g = dot(a, wg_ref[:, c])
            u = dot(a, wu_ref[:, c])
            g_ref[:, c] = g
            u_ref[:, c] = u
            hid_ref[:, c] = (g * sigmoid(g) * u).astype(bf16)

    row = lambda n: pl.BlockSpec((TM, n), lambda t: (t, 0))
    return pl.pallas_call(
        body,
        grid=(TOK // TM,),
        in_specs=[row(D), once((D, FF)), once((D, FF))],
        out_specs=[row(D), row(FF), row(FF), row(FF)],
        out_shape=[jax.ShapeDtypeStruct((TOK, n), d) for n, d in ((D, bf16), (FF, f32), (FF, f32), (FF, bf16))],
        compiler_params=PARAMS,
        cost_estimate=cost(2, FF, 130_000_000),
        name="forward_up",
    )(x, wg, wu)


def forward_down(x, hid, wd, TM=512):
    def body(x_ref, hid_ref, wd_ref, h_ref, a_ref):
        y = dot(hid_ref[...], wd_ref[...]).astype(bf16)
        h = (x_ref[...].astype(f32) + y.astype(f32)).astype(bf16)
        h_ref[...] = h
        wide = h.astype(f32)
        a_ref[...] = (wide * scale_of(wide)).astype(bf16)

    row = lambda n: pl.BlockSpec((TM, n), lambda t: (t, 0))
    return pl.pallas_call(
        body,
        grid=(TOK // TM,),
        in_specs=[row(D), row(FF), once((FF, D))],
        out_specs=[row(D), row(D)],
        out_shape=[jax.ShapeDtypeStruct((TOK, D), bf16)] * 2,
        compiler_params=PARAMS,
        cost_estimate=cost(1, FF, 60_000_000),
        name="forward_down",
    )(x, hid, wd)


def scatter_out(tmpg, tmpu, tmpd, send_ref, keep_ref):
    me = lax.axis_index("s")
    xx, core = me // 2, me % 2
    for out, oc in ((send_ref, 1 - core), (keep_ref, core)):
        for k, ox in ((0, 1 - xx), (1, xx)):
            o = 2 * ox + oc
            out[k, 0:256, :] = tmpg[o]
            out[k, 256:512, :] = tmpu[o]
            out[k, 512:640, :] = tmpd[o, :, 0:CH]
            out[k, 640:768, :] = tmpd[o, :, CH : 2 * CH]


def products(step, nt, a_v, dy_v, dg_s, du_s, hid_s, tmpg, tmpu, tmpd, send_ref, keep_ref):
    @pl.when(step == nt)
    def _():
        tmpg[...] = dot_tn(a_v[...], dg_s[...]).astype(bf16).reshape(4, 256, CH)

    @pl.when(step == nt + 1)
    def _():
        tmpu[...] = dot_tn(a_v[...], du_s[...]).astype(bf16).reshape(4, 256, CH)

    @pl.when(step == nt + 2)
    def _():
        tmpd[...] = dot_tn(hid_s[...], dy_v[...]).astype(bf16).reshape(4, 128, D)
        scatter_out(tmpg, tmpu, tmpd, send_ref, keep_ref)


def load_tiles(step, nt, TM, pairs, sems):
    copies = lambda i: [pltpu.make_async_copy(src.at[pl.ds(i * TM, TM)], dst.at[pl.ds(i * TM, TM)], sems.at[n, i]) for n, (src, dst) in enumerate(pairs)]

    @pl.when(step == 0)
    def _():
        for i in range(nt):
            for c in copies(i):
                c.start()

    @pl.when(step < nt)
    def _():
        for c in copies(step):
            c.wait()


GRADS = [jax.ShapeDtypeStruct((2, 768, CH), bf16)] * 2
GRAD_SPECS = [pl.BlockSpec((2, 768, CH), lambda t: (0, 0, 0), pipeline_mode=pl.Buffered(1))] * 2
PRODUCT_SCRATCH = (
    [pltpu.VMEM((TOK, D), bf16)] * 2
    + [pltpu.VMEM((TOK, CH), bf16)] * 3
    + [pltpu.VMEM((4, 256, CH), bf16)] * 2
    + [pltpu.VMEM((4, 128, D), bf16)]
)


def backward_top(j, a, dy, wg, wu, wd, TM=512, SUB=256):
    nt = TOK // TM

    def body(a_ref, dy_ref, *rest):
        wgs, wus, wd_ref = rest[0:4], rest[4:8], rest[8]
        dg_ref, du_ref, send_ref, keep_ref, a_v, dy_v, dg_s, du_s, hid_s, tmpg, tmpu, tmpd, wgc, wuc, sems = rest[9:]
        t = pl.program_id(0)
        load_tiles(t, nt, TM, ((a_ref, a_v), (dy_ref, dy_v)), sems)

        @pl.when(t == 0)
        def _():
            wgc[...] = jnp.concatenate([w[...] for w in wgs], axis=1)
            wuc[...] = jnp.concatenate([w[...] for w in wus], axis=1)

        @pl.when(t < nt)
        def _():
            wdc = wd_ref[...].reshape(CH, D)
            for s in range(TM // SUB):
                r = pl.ds(pl.multiple_of(t * TM + s * SUB, SUB), SUB)
                x = a_v[r, :]
                g, u = dot(x, wgc[...]), dot(x, wuc[...])
                dh = dot_nt(dy_v[r, :], wdc).astype(bf16).astype(f32)
                sig = sigmoid(g)
                silu = g * sig
                dg = (dh * u * (sig + silu - silu * sig)).astype(bf16)
                du = (dh * silu).astype(bf16)
                hid_s[r, :] = (silu * u).astype(bf16)
                dg_s[r, :] = dg
                du_s[r, :] = du
                dg_ref[s * SUB : (s + 1) * SUB, :] = dg
                du_ref[s * SUB : (s + 1) * SUB, :] = du

        products(t, nt, a_v, dy_v, dg_s, du_s, hid_s, tmpg, tmpu, tmpd, send_ref, keep_ref)

    col = [pl.BlockSpec((D, 128), functools.partial(lambda q, t: (0, q * NC + j), q), pipeline_mode=pl.Buffered(1)) for q in range(4)]
    tile = pl.BlockSpec((TM, CH), lambda t: (jnp.minimum(t, nt - 1), 0))
    return pl.pallas_call(
        body,
        grid=(nt + 3,),
        in_specs=[pl.BlockSpec(memory_space=pl.ANY)] * 2
        + col
        + col
        + [pl.BlockSpec((4, 128, D), lambda t: (0, j, 0), pipeline_mode=pl.Buffered(1))],
        out_specs=[tile, tile] + GRAD_SPECS,
        out_shape=[jax.ShapeDtypeStruct((TOK, CH), bf16)] * 2 + GRADS,
        scratch_shapes=PRODUCT_SCRATCH + [pltpu.VMEM((D, CH), bf16)] * 2 + [pltpu.SemaphoreType.DMA((2, nt))],
        compiler_params=PARAMS,
        cost_estimate=cost(6, CH, 30_000_000),
        name=f"backward_top_{j}",
    )(a, dy, *[wg] * 4, *[wu] * 4, wd.reshape(4, 640, D))


def backward_through(dgs, dus, wg, wu, h, dy, TM=256):
    def body(*refs):
        dg, du = (jnp.concatenate([refs[5 * i + j][:, 128 * q : 128 * q + 128] for q in range(4) for j in range(NC)], axis=1) for i in range(2))
        wg_ref, wu_ref, h_ref, dy_ref, out_ref = refs[10:]
        da = dot_nt(dg, wg_ref[...]).astype(bf16).astype(f32) + dot_nt(du, wu_ref[...]).astype(bf16).astype(f32)
        da = da.astype(bf16).astype(f32)
        wide = h_ref[...].astype(f32)
        scale = scale_of(wide)
        along = jnp.sum(da * wide, -1, keepdims=True) * (scale * scale * scale * (1.0 / D))
        dh = (da * scale - wide * along).astype(bf16)
        out_ref[...] = (dy_ref[...].astype(f32) + dh.astype(f32)).astype(bf16)

    row = lambda n: pl.BlockSpec((TM, n), lambda t: (t, 0))
    return pl.pallas_call(
        body,
        grid=(TOK // TM,),
        in_specs=[row(CH)] * 10 + [once((D, FF))] * 2 + [row(D)] * 2,
        out_specs=row(D),
        out_shape=jax.ShapeDtypeStruct((TOK, D), bf16),
        compiler_params=PARAMS,
        cost_estimate=cost(2, FF, 80_000_000),
        name="backward_through",
    )(*dgs, *dus, wg, wu, h, dy)


def backward_bottom(j, a, dy, gate, up, wd, TM=512, SUB=256):
    nt = TOK // TM

    def body(a_ref, dy_ref, *rest):
        gs, us, wd_ref = rest[0:4], rest[4:8], rest[8]
        send_ref, keep_ref, a_v, dy_v, dg_s, du_s, hid_s, tmpg, tmpu, tmpd, sems = rest[9:]
        t = pl.program_id(0)
        load_tiles(t, nt, TM, ((a_ref, a_v), (dy_ref, dy_v)), sems)

        @pl.when(t < nt)
        def _():
            wdc = wd_ref[...].reshape(CH, D)
            for s in range(TM // SUB):
                r = pl.ds(pl.multiple_of(t * TM + s * SUB, SUB), SUB)
                rr = slice(s * SUB, (s + 1) * SUB)
                g = jnp.concatenate([x[rr, :] for x in gs], axis=1)
                u = jnp.concatenate([x[rr, :] for x in us], axis=1)
                dh = dot_nt(dy_v[r, :], wdc).astype(bf16).astype(f32)
                sig = sigmoid(g)
                silu = g * sig
                dg_s[r, :] = (dh * u * (sig + silu - silu * sig)).astype(bf16)
                du_s[r, :] = (dh * silu).astype(bf16)
                hid_s[r, :] = (silu * u).astype(bf16)

        products(t, nt, a_v, dy_v, dg_s, du_s, hid_s, tmpg, tmpu, tmpd, send_ref, keep_ref)

    col = [pl.BlockSpec((TM, 128), functools.partial(lambda q, t: (jnp.minimum(t, nt - 1), q * NC + j), q)) for q in range(4)]
    return pl.pallas_call(
        body,
        grid=(nt + 3,),
        in_specs=[pl.BlockSpec(memory_space=pl.ANY)] * 2
        + col
        + col
        + [pl.BlockSpec((4, 128, D), lambda t: (0, j, 0), pipeline_mode=pl.Buffered(1))],
        out_specs=GRAD_SPECS,
        out_shape=GRADS,
        scratch_shapes=PRODUCT_SCRATCH + [pltpu.SemaphoreType.DMA((2, nt))],
        compiler_params=PARAMS,
        cost_estimate=cost(4, CH, 30_000_000),
        name=f"backward_bottom_{j}",
    )(a, dy, *[gate] * 4, *[up] * 4, wd.reshape(4, 640, D))


def summed(send, keep):
    wide = lambda v: v.astype(f32)
    got = lax.ppermute(send, "s", [(i, i ^ 1) for i in range(4)])
    theirs = (wide(keep[0]) + wide(got[0])).astype(bf16)
    other = lax.ppermute(theirs, "s", [(i, i ^ 2) for i in range(4)])
    ours = (wide(keep[1]) + wide(got[1]) + wide(other)).astype(bf16)
    copy = lax.ppermute(ours, "r", [(0, 1), (1, 0)])
    return (wide(ours) + wide(copy)).astype(bf16)


def blocks(chunks):
    g = jnp.stack(chunks)
    two = [g[:, 256 * i : 256 * i + 256].reshape(NC, 256, 4, 128).transpose(1, 2, 0, 3).reshape(256, FF) for i in range(2)]
    return two + [g[:, 512:].reshape(NC, 2, 128, CH).transpose(0, 2, 1, 3).reshape(640, D)]


def adamw(w, m, v, g):
    m = 0.9 * m + 0.1 * g
    v = 0.95 * v + 0.05 * g * g
    step = m * lax.rsqrt(v + 1e-8) + 0.1 * w
    return (w - 0.02 * step).astype(bf16), m, v


def solution(mesh):
    def step(x, dy, *arrays):
        weights, m, v = (arrays[i : i + 3] for i in (0, 3, 6))
        x, dy = x[0], dy[0]
        full = [[lax.all_gather(w[n], "s", axis=0, tiled=True) for w in weights] for n in range(2)]
        a0, gate, up, hid = forward_up(x, full[0][0], full[0][1])
        h, a1 = forward_down(x, hid, full[0][2])
        top = [backward_top(j, a1, dy, *full[1]) for j in range(NC)]
        g1 = [summed(send, keep) for _, _, send, keep in top]
        dh = backward_through([c[0] for c in top], [c[1] for c in top], full[1][0], full[1][1], h, dy)
        g0 = [summed(*backward_bottom(j, a0, dh, gate, up, full[0][2])) for j in range(NC)]
        mine = [blocks(g0), blocks(g1)]
        gradients = [jnp.stack([mine[n][i] for n in range(2)]).astype(f32) for i in range(3)]
        squares = lax.psum(sum(jnp.sum(g * g) for g in gradients), "s")
        count = lax.psum(1, "s") * sum(g.size for g in gradients)
        factor = jnp.minimum(1.0, 0.5 * lax.rsqrt(squares / count + 1e-30))
        new = [adamw(w.astype(f32), m, v, g * factor) for w, m, v, g in zip(weights, m, v, gradients, strict=True)]
        return tuple(one[which] for which in range(3) for one in new)

    states, cut = P(("rep", "r", "s"), None, None), P(None, "s", None)
    return jax.shard_map(
        step,
        mesh=mesh,
        in_specs=(states, states) + (cut,) * 9,
        out_specs=(P("rep", "s", None),) * 9,
        check_vma=False,
    )
```

time: 952 us -> 1060 us (1.11)
  matrix products: 531 us -> 0 us
  Pallas kernels: 0 us -> 493 us
  local copies, waits for them, and re-layouts: 36.4 us -> 104 us
  waiting for transfers between devices: 298 us -> 346 us
  starting transfers between devices: 0.53 us -> 22.1 us
  other arithmetic: 54.9 us -> 65.6 us
    dot_general x15 -> x0, matrix products: 531 us -> none  [the longest x5 193 us: layer(): up = jnp.dot(a, w['w_up'], preferred_element_type=jnp.float32)]
    pallas_call x0 -> x13, Pallas kernels: none -> 493 us  [the longest x5 186 us: backward_top(): pl.pallas_call(body, grid=(nt + 3,), in_specs=[pl.BlockSpec(memory_space=...]
    ppermute x0 -> x30, waiting for transfers between devices: none -> 226 us  [the longest x10 145 us: summed(): other = lax.ppermute(theirs, 's', [(i, i ^ 2) for i in range(4)])]
    psum x1 -> x0, waiting for transfers between devices: 184 us -> none  [summed(): lax.psum(lax.psum_scatter(term, 's', scatter_dimension=0, tiled=True), 'r')]
    all_gather x6, waiting for transfers between devices: 34.5 us -> 119 us  [step(): lax.all_gather(w[n], 's', axis=0, tiled=True)]
    reduce_scatter x6 -> x0, waiting for transfers between devices: 77.8 us -> none  [summed(): lax.psum_scatter(term, 's', scatter_dimension=0, tiled=True)]
    unnamed x34 -> x44, local copies, waits for them, and re-layouts: 27.7 us -> 64.5 us
    convert_element_type x2 -> x23, other arithmetic: 27.9 us -> 51.1 us  [the longest x3 28.8 us: adamw(): return ((w - 0.02 * step).astype(bf16), m, v)]
  transfers between devices with their start and end apart: 13 -> 36, of which waited for: 7 -> 20; matrix products, arithmetic and copies ran while one was open for 44% -> 6% of each run, Pallas kernels for 0% -> 14%
where the time goes in v1:
time: 1060 us
  Pallas kernels  493 us (47%)
  waiting for transfers between devices  346 us (33%)
  local copies, waits for them, and re-layouts  104 us (10%)
  other arithmetic  65.6 us (6%)
  starting transfers between devices  22.1 us (2%)
  between operations  17.5 us (2%)
    pallas_call x5, Pallas kernels, backward_top(): pl.pallas_call(body, grid=(nt + 3,), in_specs=[pl.BlockSpec(memory_space=...  186 us
    pallas_call x5, Pallas kernels, backward_bottom(): pl.pallas_call(body, grid=(nt + 3,), in_specs=[pl.BlockSpec(memory_space=...  161 us
    ppermute x10, waiting for transfers between devices, summed(): other = lax.ppermute(theirs, 's', [(i, i ^ 2) for i in range(4)])  145 us
    all_gather x6, waiting for transfers between devices, step(): lax.all_gather(w[n], 's', axis=0, tiled=True)  119 us
    ppermute x10, waiting for transfers between devices, summed(): copy = lax.ppermute(ours, 'r', [(0, 1), (1, 0)])  80.4 us
    unnamed x44, local copies, waits for them, and re-layouts  64.5 us
    pallas_call x1, Pallas kernels, backward_through(): pl.pallas_call(body, grid=(TOK // TM,), in_specs=[row(CH)] * 10 + [once((...  59.6 us
    pallas_call x1, Pallas kernels, forward_up(): pl.pallas_call(body, grid=(TOK // TM,), in_specs=[row(D), once((D, FF)),...  56 us
  transfers between devices with their start and end apart: 36, of which 20 were waited for; matrix products, arithmetic and copies ran while one was open for 6% of the time, Pallas kernels for 14%

profile of v1, /device:TPU:0, one launch (start us, length us, event | category | flops | bytes accessed | tf_op | source)
XLA Modules:
  0.0 1055.5 jit_solution(10189328561822995673)
XLA Ops:
  51.3 39.7 %all-gather.15.cloned.1.call-done = bf16[1,1024,2560]{2,1,0:T(8,128)(2,1)} async-done(((bf16[1,256,2560]{2,1,0:T(8,128)(2,1)}), bf16[1,1024,2560]{2,1,0:T(8,128)(2,1)}) %all-gather.15.cloned.1.call-update) | async-done | bytes 5242896 | tf_op jit(solution)/shard_map/all_gather | solution.py:291
  91.0 56.0 %forward_up.1 = (bf16[4096,1024]{1,0:T(8,128)(2,1)}, f32[4096,2560]{1,0:T(8,128)}, f32[4096,2560]{1,0:T(8,128)}, bf16[4096,2560]{1,0:T(8,128)(2,1)}) custom-call(bf16[4096,1024]{1,0:T(8,128)(2,1)} %bitcast.143, bf16[1024,2560]{1,0:T(8,128)(2,1)} %bitcast.193, bf16[1024,2560]{1,0:T(8,128)(2,1)} %bitcast.194), custom_call_target="tpu_custom_call" | custom-call | flops 42949672960 | bytes 130000000 | tf_op jit(solution)/shard_map/forward_up/pallas_call | solution.py:59
  147.0 30.6 %forward_down.1 = (bf16[4096,1024]{1,0:T(8,128)(2,1)}, bf16[4096,1024]{1,0:T(8,128)(2,1)}) custom-call(bf16[4096,1024]{1,0:T(8,128)(2,1)} %bitcast.144, bf16[4096,2560]{1,0:T(8,128)(2,1)} %get-tuple-element.46.hid_ref, bf16[2560,1024]{1,0:T(8,128)(2,1)} %bitcast.127), custom_call_target="tpu_custom_call" | custom-call | flops 21474836480 | bytes 60000000 | tf_op jit(solution)/shard_map/forward_down/pallas_call | solution.py:80
  177.7 31.6 %all-gather.21.cloned.1.call-done = bf16[1,1024,2560]{2,1,0:T(8,128)(2,1)} async-done(((bf16[1,256,2560]{2,1,0:T(8,128)(2,1)}), bf16[1,1024,2560]{2,1,0:T(8,128)(2,1)}) %all-gather.21.cloned.1.call-update) | async-done | bytes 5242896 | tf_op jit(solution)/shard_map/all_gather | solution.py:291
  209.2 39.0 %all-gather.23.cloned.1.call-done = bf16[1,2560,1024]{2,1,0:T(8,128)(2,1)} async-done(((bf16[1,640,1024]{2,1,0:T(8,128)(2,1)}), bf16[1,2560,1024]{2,1,0:T(8,128)(2,1)}) %all-gather.23.cloned.1.call-update) | async-done | bytes 5242896 | tf_op jit(solution)/shard_map/all_gather | solution.py:291
  248.2 37.4 %backward_top_0.1 = (bf16[4096,512]{1,0:T(8,128)(2,1)}, bf16[4096,512]{1,0:T(8,128)(2,1)}, bf16[2,768,512]{2,1,0:T(8,128)(2,1)}, bf16[2,768,512]{2,1,0:T(8,128)(2,1)}) custom-call(bf16[4096,1024]{1,0:T(8,128)(2,1)} %get-tuple-element.47.a_ref, bf16[4096,1024]{1,0:T(8,128)(2,1)} %bitcast.145, bf16[1024,2560]{1,0:T(8,128)(2,1)} %bitcast.151, ...), custom_call_target="tpu_custom_call" | custom-call | flops 25769803776 | bytes 30000000 | tf_op jit(solution)/shard_map/backward_top_0/pallas_call | solution.py:180
  285.6 37.2 %backward_top_1.1 = (bf16[4096,512]{1,0:T(8,128)(2,1)}, bf16[4096,512]{1,0:T(8,128)(2,1)}, bf16[2,768,512]{2,1,0:T(8,128)(2,1)}, bf16[2,768,512]{2,1,0:T(8,128)(2,1)}) custom-call(bf16[4096,1024]{1,0:T(8,128)(2,1)} %get-tuple-element.47.a_ref, bf16[4096,1024]{1,0:T(8,128)(2,1)} %bitcast.146, bf16[1024,2560]{1,0:T(8,128)(2,1)} %bitcast.155, ...), custom_call_target="tpu_custom_call" | custom-call | flops 25769803776 | bytes 30000000 | tf_op jit(solution)/shard_map/backward_top_1/pallas_call | solution.py:180
  322.8 37.2 %backward_top_2.1 = (bf16[4096,512]{1,0:T(8,128)(2,1)}, bf16[4096,512]{1,0:T(8,128)(2,1)}, bf16[2,768,512]{2,1,0:T(8,128)(2,1)}, bf16[2,768,512]{2,1,0:T(8,128)(2,1)}) custom-call(bf16[4096,1024]{1,0:T(8,128)(2,1)} %get-tuple-element.47.a_ref, bf16[4096,1024]{1,0:T(8,128)(2,1)} %bitcast.147, bf16[1024,2560]{1,0:T(8,128)(2,1)} %bitcast.159, ...), custom_call_target="tpu_custom_call" | custom-call | flops 25769803776 | bytes 30000000 | tf_op jit(solution)/shard_map/backward_top_2/pallas_call | solution.py:180
  360.0 37.5 %backward_top_3.1 = (bf16[4096,512]{1,0:T(8,128)(2,1)}, bf16[4096,512]{1,0:T(8,128)(2,1)}, bf16[2,768,512]{2,1,0:T(8,128)(2,1)}, bf16[2,768,512]{2,1,0:T(8,128)(2,1)}) custom-call(bf16[4096,1024]{1,0:T(8,128)(2,1)} %get-tuple-element.47.a_ref, bf16[4096,1024]{1,0:T(8,128)(2,1)} %bitcast.148, bf16[1024,2560]{1,0:T(8,128)(2,1)} %bitcast.163, ...), custom_call_target="tpu_custom_call" | custom-call | flops 25769803776 | bytes 30000000 | tf_op jit(solution)/shard_map/backward_top_3/pallas_call | solution.py:180
  397.5 37.2 %backward_top_4.1 = (bf16[4096,512]{1,0:T(8,128)(2,1)}, bf16[4096,512]{1,0:T(8,128)(2,1)}, bf16[2,768,512]{2,1,0:T(8,128)(2,1)}, bf16[2,768,512]{2,1,0:T(8,128)(2,1)}) custom-call(bf16[4096,1024]{1,0:T(8,128)(2,1)} %get-tuple-element.47.a_ref, bf16[4096,1024]{1,0:T(8,128)(2,1)} %bitcast.149, bf16[1024,2560]{1,0:T(8,128)(2,1)} %bitcast.167, ...), custom_call_target="tpu_custom_call" | custom-call | flops 25769803776 | bytes 30000000 | tf_op jit(solution)/shard_map/backward_top_4/pallas_call | solution.py:180
  434.6 59.6 %backward_through.1.dy_ref = bf16[4096,1024]{1,0:T(8,128)(2,1)} custom-call(bf16[4096,512]{1,0:T(8,128)(2,1)} %get-tuple-element.48.refs_0_, bf16[4096,512]{1,0:T(8,128)(2,1)} %get-tuple-element.49.refs_1_, bf16[4096,512]{1,0:T(8,128)(2,1)} %get-tuple-element.50.refs_2_, bf16[4096,512]{1,0:T(8,128)(2,1)} %get-tuple-element.51.refs_3_, ...), custom_call_target="tpu_custom_call" | custom-call | flops 42949672960 | bytes 80000000 | tf_op jit(solution)/shard_map/backward_through/pallas_call | solution.py:209
  494.2 31.9 %backward_bottom_0.1 = (bf16[2,768,512]{2,1,0:T(8,128)(2,1)}, bf16[2,768,512]{2,1,0:T(8,128)(2,1)}) custom-call(bf16[4096,1024]{1,0:T(8,128)(2,1)} %get-tuple-element.45.a_ref, bf16[4096,1024]{1,0:T(8,128)(2,1)} %backward_through.1.dy_ref, f32[4096,2560]{1,0:T(8,128)} %get-tuple-element.59.rest_0_.rest_1_.rest_2_.rest_3_, ...), custom_call_target="tpu_custom_call" | custom-call | flops 17179869184 | bytes 30000000 | tf_op jit(solution)/shard_map/backward_bottom_0/pallas_call | solution.py:248
  526.1 32.3 %backward_bottom_1.1 = (bf16[2,768,512]{2,1,0:T(8,128)(2,1)}, bf16[2,768,512]{2,1,0:T(8,128)(2,1)}) custom-call(bf16[4096,1024]{1,0:T(8,128)(2,1)} %get-tuple-element.45.a_ref, bf16[4096,1024]{1,0:T(8,128)(2,1)} %backward_through.1.dy_ref, f32[4096,2560]{1,0:T(8,128)} %get-tuple-element.59.rest_0_.rest_1_.rest_2_.rest_3_, ...), custom_call_target="tpu_custom_call" | custom-call | flops 17179869184 | bytes 30000000 | tf_op jit(solution)/shard_map/backward_bottom_1/pallas_call | solution.py:248
  558.4 32.1 %backward_bottom_2.1 = (bf16[2,768,512]{2,1,0:T(8,128)(2,1)}, bf16[2,768,512]{2,1,0:T(8,128)(2,1)}) custom-call(bf16[4096,1024]{1,0:T(8,128)(2,1)} %get-tuple-element.45.a_ref, bf16[4096,1024]{1,0:T(8,128)(2,1)} %backward_through.1.dy_ref, f32[4096,2560]{1,0:T(8,128)} %get-tuple-element.59.rest_0_.rest_1_.rest_2_.rest_3_, ...), custom_call_target="tpu_custom_call" | custom-call | flops 17179869184 | bytes 30000000 | tf_op jit(solution)/shard_map/backward_bottom_2/pallas_call | solution.py:248
  591.8 32.1 %backward_bottom_3.1 = (bf16[2,768,512]{2,1,0:T(8,128)(2,1)}, bf16[2,768,512]{2,1,0:T(8,128)(2,1)}) custom-call(bf16[4096,1024]{1,0:T(8,128)(2,1)} %get-tuple-element.45.a_ref, bf16[4096,1024]{1,0:T(8,128)(2,1)} %backward_through.1.dy_ref, f32[4096,2560]{1,0:T(8,128)} %get-tuple-element.59.rest_0_.rest_1_.rest_2_.rest_3_, ...), custom_call_target="tpu_custom_call" | custom-call | flops 17179869184 | bytes 30000000 | tf_op jit(solution)/shard_map/backward_bottom_3/pallas_call | solution.py:248
  625.3 32.4 %backward_bottom_4.1 = (bf16[2,768,512]{2,1,0:T(8,128)(2,1)}, bf16[2,768,512]{2,1,0:T(8,128)(2,1)}) custom-call(bf16[4096,1024]{1,0:T(8,128)(2,1)} %get-tuple-element.45.a_ref, bf16[4096,1024]{1,0:T(8,128)(2,1)} %backward_through.1.dy_ref, f32[4096,2560]{1,0:T(8,128)} %get-tuple-element.59.rest_0_.rest_1_.rest_2_.rest_3_, ...), custom_call_target="tpu_custom_call" | custom-call | flops 17179869184 | bytes 30000000 | tf_op jit(solution)/shard_map/backward_bottom_4/pallas_call | solution.py:248
  673.4 13.5 %collective-permute-done.16 = bf16[768,512]{1,0:T(8,128)(2,1)S(1)} collective-permute-done((bf16[768,512]{1,0:T(8,128)(2,1)S(1)}, bf16[768,512]{1,0:T(8,128)(2,1)S(1)}, u32[]{:S(2)}, u32[]{:S(2)}) %collective-permute-start.16) | collective-permute-done | bytes 786464 | tf_op jit(solution)/shard_map/ppermute | solution.py:268
  687.6 16.2 %collective-permute-done.19 = bf16[768,512]{1,0:T(8,128)(2,1)S(1)} collective-permute-done((bf16[768,512]{1,0:T(8,128)(2,1)S(1)}, bf16[768,512]{1,0:T(8,128)(2,1)S(1)}, u32[]{:S(2)}, u32[]{:S(2)}) %collective-permute-start.19) | collective-permute-done | bytes 786464 | tf_op jit(solution)/shard_map/ppermute | solution.py:268
  705.6 15.0 %collective-permute-done.22 = bf16[768,512]{1,0:T(8,128)(2,1)S(1)} collective-permute-done((bf16[768,512]{1,0:T(8,128)(2,1)S(1)}, bf16[768,512]{1,0:T(8,128)(2,1)S(1)}, u32[]{:S(2)}, u32[]{:S(2)}) %collective-permute-start.22) | collective-permute-done | bytes 786464 | tf_op jit(solution)/shard_map/ppermute | solution.py:268
  722.4 15.0 %collective-permute-done.25 = bf16[768,512]{1,0:T(8,128)(2,1)S(1)} collective-permute-done((bf16[768,512]{1,0:T(8,128)(2,1)S(1)}, bf16[768,512]{1,0:T(8,128)(2,1)S(1)}, u32[]{:S(2)}, u32[]{:S(2)}) %collective-permute-start.25) | collective-permute-done | bytes 786464 | tf_op jit(solution)/shard_map/ppermute | solution.py:268
  739.3 15.0 %collective-permute-done.28 = bf16[768,512]{1,0:T(8,128)(2,1)S(1)} collective-permute-done((bf16[768,512]{1,0:T(8,128)(2,1)S(1)}, bf16[768,512]{1,0:T(8,128)(2,1)S(1)}, u32[]{:S(2)}, u32[]{:S(2)}) %collective-permute-start.28) | collective-permute-done | bytes 786464 | tf_op jit(solution)/shard_map/ppermute | solution.py:268
  756.1 15.0 %collective-permute-done.1 = bf16[768,512]{1,0:T(8,128)(2,1)S(1)} collective-permute-done((bf16[768,512]{1,0:T(8,128)(2,1)S(1)}, bf16[768,512]{1,0:T(8,128)(2,1)S(1)}, u32[]{:S(2)}, u32[]{:S(2)}) %collective-permute-start.1) | collective-permute-done | bytes 786464 | tf_op jit(solution)/shard_map/ppermute | solution.py:268
  774.1 13.9 %collective-permute-done.4 = bf16[768,512]{1,0:T(8,128)(2,1)S(1)} collective-permute-done((bf16[768,512]{1,0:T(8,128)(2,1)S(1)}, bf16[768,512]{1,0:T(8,128)(2,1)S(1)}, u32[]{:S(2)}, u32[]{:S(2)}) %collective-permute-start.4) | collective-permute-done | bytes 786464 | tf_op jit(solution)/shard_map/ppermute | solution.py:268
  790.7 14.2 %collective-permute-done.7 = bf16[768,512]{1,0:T(8,128)(2,1)S(1)} collective-permute-done((bf16[768,512]{1,0:T(8,128)(2,1)S(1)}, bf16[768,512]{1,0:T(8,128)(2,1)S(1)}, u32[]{:S(2)}, u32[]{:S(2)}) %collective-permute-start.7) | collective-permute-done | bytes 786464 | tf_op jit(solution)/shard_map/ppermute | solution.py:268
  807.6 14.2 %collective-permute-done.10 = bf16[768,512]{1,0:T(8,128)(2,1)S(1)} collective-permute-done((bf16[768,512]{1,0:T(8,128)(2,1)S(1)}, bf16[768,512]{1,0:T(8,128)(2,1)S(1)}, u32[]{:S(2)}, u32[]{:S(2)}) %collective-permute-start.10) | collective-permute-done | bytes 786464 | tf_op jit(solution)/shard_map/ppermute | solution.py:268
  824.4 13.4 %collective-permute-done.13 = bf16[768,512]{1,0:T(8,128)(2,1)S(1)} collective-permute-done((bf16[768,512]{1,0:T(8,128)(2,1)S(1)}, bf16[768,512]{1,0:T(8,128)(2,1)S(1)}, u32[]{:S(2)}, u32[]{:S(2)}) %collective-permute-start.13) | collective-permute-done | bytes 786464 | tf_op jit(solution)/shard_map/ppermute | solution.py:268
  845.6 12.6 %collective-permute-done.29 = bf16[768,512]{1,0:T(8,128)(2,1)S(1)} collective-permute-done((bf16[768,512]{1,0:T(8,128)(2,1)S(1)}, bf16[768,512]{1,0:T(8,128)(2,1)S(1)}, u32[]{:S(2)}, u32[]{:S(2)}) %collective-permute-start.29) | collective-permute-done | bytes 786464 | tf_op jit(solution)/shard_map/ppermute | solution.py:270
  876.4 15.5 %collective-permute-done.5 = bf16[768,512]{1,0:T(8,128)(2,1)} collective-permute-done((bf16[768,512]{1,0:T(8,128)(2,1)}, bf16[768,512]{1,0:T(8,128)(2,1)}, u32[]{:S(2)}, u32[]{:S(2)}) %collective-permute-start.5) | collective-permute-done | bytes 786464 | tf_op jit(solution)/shard_map/ppermute | solution.py:270
  893.5 15.3 %collective-permute-done.8 = bf16[768,512]{1,0:T(8,128)(2,1)} collective-permute-done((bf16[768,512]{1,0:T(8,128)(2,1)}, bf16[768,512]{1,0:T(8,128)(2,1)}, u32[]{:S(2)}, u32[]{:S(2)}) %collective-permute-start.8) | collective-permute-done | bytes 786464 | tf_op jit(solution)/shard_map/ppermute | solution.py:270
  910.4 15.3 %collective-permute-done.11 = bf16[768,512]{1,0:T(8,128)(2,1)} collective-permute-done((bf16[768,512]{1,0:T(8,128)(2,1)}, bf16[768,512]{1,0:T(8,128)(2,1)}, u32[]{:S(2)}, u32[]{:S(2)}) %collective-permute-start.11) | collective-permute-done | bytes 786464 | tf_op jit(solution)/shard_map/ppermute | solution.py:270
  927.2 13.7 %collective-permute-done.14 = bf16[768,512]{1,0:T(8,128)(2,1)} collective-permute-done((bf16[768,512]{1,0:T(8,128)(2,1)}, bf16[768,512]{1,0:T(8,128)(2,1)}, u32[]{:S(2)}, u32[]{:S(2)}) %collective-permute-start.14) | collective-permute-done | bytes 786464 | tf_op jit(solution)/shard_map/ppermute | solution.py:270
  987.4 9.7 fusion.8
  (156 shorter events, 206.9 us)
Async XLA Ops:
  7.2 44.1 %all-gather.13.cloned.1.call-start = ((), (), s32[]{:S(2)}) async-start(), calls=%async_computation | async-start | bytes 6553600 | tf_op jit(solution)/shard_map/all_gather | solution.py:291
  10.8 80.2 %all-gather.15.cloned.1.call-start = ((), (), s32[]{:S(2)}) async-start(), calls=%async_computation.1 | async-start | bytes 6553600 | tf_op jit(solution)/shard_map/all_gather | solution.py:291
  12.5 134.5 %all-gather.17.cloned.1.call-start = ((), (), s32[]{:S(2)}) async-start(), calls=%async_computation.2 | async-start | bytes 6553600 | tf_op jit(solution)/shard_map/all_gather | solution.py:291
  16.0 161.6 %all-gather.19.cloned.1.call-start = ((), (), s32[]{:S(2)}) async-start(), calls=%async_computation.3 | async-start | bytes 6553600 | tf_op jit(solution)/shard_map/all_gather | solution.py:291
  16.6 192.6 %all-gather.21.cloned.1.call-start = ((), (), s32[]{:S(2)}) async-start(), calls=%async_computation.4 | async-start | bytes 6553600 | tf_op jit(solution)/shard_map/all_gather | solution.py:291
  17.2 231.0 %all-gather.23.cloned.1.call-start = ((), (), s32[]{:S(2)}) async-start(), calls=%async_computation.5 | async-start | bytes 6553600 | tf_op jit(solution)/shard_map/all_gather | solution.py:291
  590.5 33.4 %collective-permute-start.15 = (bf16[2,768,512]{2,1,0:T(8,128)(2,1)}, bf16[2,768,512]{2,1,0:T(8,128)(2,1)S(1)}, u32[]{:S(2)}, u32[]{:S(2)}) collective-permute-start(bf16[2,768,512]{2,1,0:T(8,128)(2,1)} %get-tuple-element.72), channel_id=1, source_target_pairs={{0,1},{1,0},{2,3},{3,2},{4,5},{5,4},{6,7},{7,6}} | collective-permute-start | bytes 4718600 | tf_op jit(solution)/shard_map/ppermute | solution.py:266
  590.8 67.0 %collective-permute-start.18 = (bf16[2,768,512]{2,1,0:T(8,128)(2,1)}, bf16[2,768,512]{2,1,0:T(8,128)(2,1)}, u32[]{:S(2)}, u32[]{:S(2)}) collective-permute-start(bf16[2,768,512]{2,1,0:T(8,128)(2,1)} %get-tuple-element.74), channel_id=1, source_target_pairs={{0,1},{1,0},{2,3},{3,2},{4,5},{5,4},{6,7},{7,6}} | collective-permute-start | bytes 4718600 | tf_op jit(solution)/shard_map/ppermute | solution.py:266
  591.0 68.5 %collective-permute-start.21 = (bf16[2,768,512]{2,1,0:T(8,128)(2,1)}, bf16[2,768,512]{2,1,0:T(8,128)(2,1)}, u32[]{:S(2)}, u32[]{:S(2)}) collective-permute-start(bf16[2,768,512]{2,1,0:T(8,128)(2,1)} %get-tuple-element.76), channel_id=1, source_target_pairs={{0,1},{1,0},{2,3},{3,2},{4,5},{5,4},{6,7},{7,6}} | collective-permute-start | bytes 4718600 | tf_op jit(solution)/shard_map/ppermute | solution.py:266
  591.3 70.1 %collective-permute-start.24 = (bf16[2,768,512]{2,1,0:T(8,128)(2,1)}, bf16[2,768,512]{2,1,0:T(8,128)(2,1)}, u32[]{:S(2)}, u32[]{:S(2)}) collective-permute-start(bf16[2,768,512]{2,1,0:T(8,128)(2,1)} %get-tuple-element.78), channel_id=1, source_target_pairs={{0,1},{1,0},{2,3},{3,2},{4,5},{5,4},{6,7},{7,6}} | collective-permute-start | bytes 4718600 | tf_op jit(solution)/shard_map/ppermute | solution.py:266
  591.6 71.6 %collective-permute-start.27 = (bf16[2,768,512]{2,1,0:T(8,128)(2,1)}, bf16[2,768,512]{2,1,0:T(8,128)(2,1)}, u32[]{:S(2)}, u32[]{:S(2)}) collective-permute-start(bf16[2,768,512]{2,1,0:T(8,128)(2,1)} %get-tuple-element.80), channel_id=1, source_target_pairs={{0,1},{1,0},{2,3},{3,2},{4,5},{5,4},{6,7},{7,6}} | collective-permute-start | bytes 4718600 | tf_op jit(solution)/shard_map/ppermute | solution.py:266
  625.0 41.4 %collective-permute-start = (bf16[2,768,512]{2,1,0:T(8,128)(2,1)}, bf16[2,768,512]{2,1,0:T(8,128)(2,1)}, u32[]{:S(2)}, u32[]{:S(2)}) collective-permute-start(bf16[2,768,512]{2,1,0:T(8,128)(2,1)} %get-tuple-element.62), channel_id=1, source_target_pairs={{0,1},{1,0},{2,3},{3,2},{4,5},{5,4},{6,7},{7,6}} | collective-permute-start | bytes 4718600 | tf_op jit(solution)/shard_map/ppermute | solution.py:266
  666.4 20.4 %collective-permute-start.16 = (bf16[768,512]{1,0:T(8,128)(2,1)S(1)}, bf16[768,512]{1,0:T(8,128)(2,1)S(1)}, u32[]{:S(2)}, u32[]{:S(2)}) collective-permute-start(bf16[768,512]{1,0:T(8,128)(2,1)S(1)} %fusion.46), channel_id=1, source_target_pairs={{0,2},{1,3},{2,0},{3,1},{4,6},{5,7},{6,4},{7,5}} | collective-permute-start | bytes 2359304 | tf_op jit(solution)/shard_map/ppermute | solution.py:268
  668.3 35.5 %collective-permute-start.19 = (bf16[768,512]{1,0:T(8,128)(2,1)S(1)}, bf16[768,512]{1,0:T(8,128)(2,1)S(1)}, u32[]{:S(2)}, u32[]{:S(2)}) collective-permute-start(bf16[768,512]{1,0:T(8,128)(2,1)S(1)} %fusion.49), channel_id=1, source_target_pairs={{0,2},{1,3},{2,0},{3,1},{4,6},{5,7},{6,4},{7,5}} | collective-permute-start | bytes 2359304 | tf_op jit(solution)/shard_map/ppermute | solution.py:268
  670.1 50.4 %collective-permute-start.22 = (bf16[768,512]{1,0:T(8,128)(2,1)S(1)}, bf16[768,512]{1,0:T(8,128)(2,1)S(1)}, u32[]{:S(2)}, u32[]{:S(2)}) collective-permute-start(bf16[768,512]{1,0:T(8,128)(2,1)S(1)} %fusion.52), channel_id=1, source_target_pairs={{0,2},{1,3},{2,0},{3,1},{4,6},{5,7},{6,4},{7,5}} | collective-permute-start | bytes 2359304 | tf_op jit(solution)/shard_map/ppermute | solution.py:268
  670.9 66.6 %collective-permute-start.25 = (bf16[768,512]{1,0:T(8,128)(2,1)S(1)}, bf16[768,512]{1,0:T(8,128)(2,1)S(1)}, u32[]{:S(2)}, u32[]{:S(2)}) collective-permute-start(bf16[768,512]{1,0:T(8,128)(2,1)S(1)} %fusion.55), channel_id=1, source_target_pairs={{0,2},{1,3},{2,0},{3,1},{4,6},{5,7},{6,4},{7,5}} | collective-permute-start | bytes 2359304 | tf_op jit(solution)/shard_map/ppermute | solution.py:268
  672.7 81.6 %collective-permute-start.28 = (bf16[768,512]{1,0:T(8,128)(2,1)S(1)}, bf16[768,512]{1,0:T(8,128)(2,1)S(1)}, u32[]{:S(2)}, u32[]{:S(2)}) collective-permute-start(bf16[768,512]{1,0:T(8,128)(2,1)S(1)} %fusion.58), channel_id=1, source_target_pairs={{0,2},{1,3},{2,0},{3,1},{4,6},{5,7},{6,4},{7,5}} | collective-permute-start | bytes 2359304 | tf_op jit(solution)/shard_map/ppermute | solution.py:268
  686.9 84.3 %collective-permute-start.1 = (bf16[768,512]{1,0:T(8,128)(2,1)S(1)}, bf16[768,512]{1,0:T(8,128)(2,1)S(1)}, u32[]{:S(2)}, u32[]{:S(2)}) collective-permute-start(bf16[768,512]{1,0:T(8,128)(2,1)S(1)} %fusion.31), channel_id=1, source_target_pairs={{0,2},{1,3},{2,0},{3,1},{4,6},{5,7},{6,4},{7,5}} | collective-permute-start | bytes 2359304 | tf_op jit(solution)/shard_map/ppermute | solution.py:268
  703.7 84.3 %collective-permute-start.4 = (bf16[768,512]{1,0:T(8,128)(2,1)S(1)}, bf16[768,512]{1,0:T(8,128)(2,1)S(1)}, u32[]{:S(2)}, u32[]{:S(2)}) collective-permute-start(bf16[768,512]{1,0:T(8,128)(2,1)S(1)} %fusion.34), channel_id=1, source_target_pairs={{0,2},{1,3},{2,0},{3,1},{4,6},{5,7},{6,4},{7,5}} | collective-permute-start | bytes 2359304 | tf_op jit(solution)/shard_map/ppermute | solution.py:268
  720.6 84.3 %collective-permute-start.7 = (bf16[768,512]{1,0:T(8,128)(2,1)S(1)}, bf16[768,512]{1,0:T(8,128)(2,1)S(1)}, u32[]{:S(2)}, u32[]{:S(2)}) collective-permute-start(bf16[768,512]{1,0:T(8,128)(2,1)S(1)} %fusion.37), channel_id=1, source_target_pairs={{0,2},{1,3},{2,0},{3,1},{4,6},{5,7},{6,4},{7,5}} | collective-permute-start | bytes 2359304 | tf_op jit(solution)/shard_map/ppermute | solution.py:268
  737.4 84.3 %collective-permute-start.10 = (bf16[768,512]{1,0:T(8,128)(2,1)S(1)}, bf16[768,512]{1,0:T(8,128)(2,1)S(1)}, u32[]{:S(2)}, u32[]{:S(2)}) collective-permute-start(bf16[768,512]{1,0:T(8,128)(2,1)S(1)} %fusion.40), channel_id=1, source_target_pairs={{0,2},{1,3},{2,0},{3,1},{4,6},{5,7},{6,4},{7,5}} | collective-permute-start | bytes 2359304 | tf_op jit(solution)/shard_map/ppermute | solution.py:268
  754.3 83.5 %collective-permute-start.13 = (bf16[768,512]{1,0:T(8,128)(2,1)S(1)}, bf16[768,512]{1,0:T(8,128)(2,1)S(1)}, u32[]{:S(2)}, u32[]{:S(2)}) collective-permute-start(bf16[768,512]{1,0:T(8,128)(2,1)S(1)} %fusion.43), channel_id=1, source_target_pairs={{0,2},{1,3},{2,0},{3,1},{4,6},{5,7},{6,4},{7,5}} | collective-permute-start | bytes 2359304 | tf_op jit(solution)/shard_map/ppermute | solution.py:268
  771.1 69.4 %collective-permute-start.17 = (bf16[768,512]{1,0:T(8,128)(2,1)S(1)}, bf16[768,512]{1,0:T(8,128)(2,1)S(1)}, u32[]{:S(2)}, u32[]{:S(2)}) collective-permute-start(bf16[768,512]{1,0:T(8,128)(2,1)S(1)} %fusion.25), channel_id=1, source_target_pairs={{0,4},{4,0},{1,5},{5,1},{2,6},{6,2},{3,7},{7,3}} | collective-permute-start | bytes 2359304 | tf_op jit(solution)/shard_map/ppermute | solution.py:270
  788.0 53.3 %collective-permute-start.20 = (bf16[768,512]{1,0:T(8,128)(2,1)S(1)}, bf16[768,512]{1,0:T(8,128)(2,1)S(1)}, u32[]{:S(2)}, u32[]{:S(2)}) collective-permute-start(bf16[768,512]{1,0:T(8,128)(2,1)S(1)} %fusion.24), channel_id=1, source_target_pairs={{0,4},{4,0},{1,5},{5,1},{2,6},{6,2},{3,7},{7,3}} | collective-permute-start | bytes 2359304 | tf_op jit(solution)/shard_map/ppermute | solution.py:270
  804.9 38.2 %collective-permute-start.23 = (bf16[768,512]{1,0:T(8,128)(2,1)S(1)}, bf16[768,512]{1,0:T(8,128)(2,1)S(1)}, u32[]{:S(2)}, u32[]{:S(2)}) collective-permute-start(bf16[768,512]{1,0:T(8,128)(2,1)S(1)} %fusion.23), channel_id=1, source_target_pairs={{0,4},{4,0},{1,5},{5,1},{2,6},{6,2},{3,7},{7,3}} | collective-permute-start | bytes 2359304 | tf_op jit(solution)/shard_map/ppermute | solution.py:270
  821.7 22.2 %collective-permute-start.26 = (bf16[768,512]{1,0:T(8,128)(2,1)S(1)}, bf16[768,512]{1,0:T(8,128)(2,1)S(1)}, u32[]{:S(2)}, u32[]{:S(2)}) collective-permute-start(bf16[768,512]{1,0:T(8,128)(2,1)S(1)} %fusion.22), channel_id=1, source_target_pairs={{0,4},{4,0},{1,5},{5,1},{2,6},{6,2},{3,7},{7,3}} | collective-permute-start | bytes 2359304 | tf_op jit(solution)/shard_map/ppermute | solution.py:270
  837.8 20.4 %collective-permute-start.29 = (bf16[768,512]{1,0:T(8,128)(2,1)S(1)}, bf16[768,512]{1,0:T(8,128)(2,1)S(1)}, u32[]{:S(2)}, u32[]{:S(2)}) collective-permute-start(bf16[768,512]{1,0:T(8,128)(2,1)S(1)} %fusion.21), channel_id=1, source_target_pairs={{0,4},{4,0},{1,5},{5,1},{2,6},{6,2},{3,7},{7,3}} | collective-permute-start | bytes 2359304 | tf_op jit(solution)/shard_map/ppermute | solution.py:270
  840.5 34.5 %collective-permute-start.2 = (bf16[768,512]{1,0:T(8,128)(2,1)S(1)}, bf16[768,512]{1,0:T(8,128)(2,1)}, u32[]{:S(2)}, u32[]{:S(2)}) collective-permute-start(bf16[768,512]{1,0:T(8,128)(2,1)S(1)} %fusion.30), channel_id=1, source_target_pairs={{0,4},{4,0},{1,5},{5,1},{2,6},{6,2},{3,7},{7,3}} | collective-permute-start | bytes 2359304 | tf_op jit(solution)/shard_map/ppermute | solution.py:270
  841.4 50.6 %collective-permute-start.5 = (bf16[768,512]{1,0:T(8,128)(2,1)}, bf16[768,512]{1,0:T(8,128)(2,1)}, u32[]{:S(2)}, u32[]{:S(2)}) collective-permute-start(bf16[768,512]{1,0:T(8,128)(2,1)} %fusion.29), channel_id=1, source_target_pairs={{0,4},{4,0},{1,5},{5,1},{2,6},{6,2},{3,7},{7,3}} | collective-permute-start | bytes 2359304 | tf_op jit(solution)/shard_map/ppermute | solution.py:270
  843.1 65.7 %collective-permute-start.8 = (bf16[768,512]{1,0:T(8,128)(2,1)}, bf16[768,512]{1,0:T(8,128)(2,1)}, u32[]{:S(2)}, u32[]{:S(2)}) collective-permute-start(bf16[768,512]{1,0:T(8,128)(2,1)} %fusion.28), channel_id=1, source_target_pairs={{0,4},{4,0},{1,5},{5,1},{2,6},{6,2},{3,7},{7,3}} | collective-permute-start | bytes 2359304 | tf_op jit(solution)/shard_map/ppermute | solution.py:270
  843.9 81.7 %collective-permute-start.11 = (bf16[768,512]{1,0:T(8,128)(2,1)}, bf16[768,512]{1,0:T(8,128)(2,1)}, u32[]{:S(2)}, u32[]{:S(2)}) collective-permute-start(bf16[768,512]{1,0:T(8,128)(2,1)} %fusion.27), channel_id=1, source_target_pairs={{0,4},{4,0},{1,5},{5,1},{2,6},{6,2},{3,7},{7,3}} | collective-permute-start | bytes 2359304 | tf_op jit(solution)/shard_map/ppermute | solution.py:270
  858.2 82.7 %collective-permute-start.14 = (bf16[768,512]{1,0:T(8,128)(2,1)}, bf16[768,512]{1,0:T(8,128)(2,1)}, u32[]{:S(2)}, u32[]{:S(2)}) collective-permute-start(bf16[768,512]{1,0:T(8,128)(2,1)} %fusion.26), channel_id=1, source_target_pairs={{0,4},{4,0},{1,5},{5,1},{2,6},{6,2},{3,7},{7,3}} | collective-permute-start | bytes 2359304 | tf_op jit(solution)/shard_map/ppermute | solution.py:270
  (20 other events, 120.6 us)
Sparse Core Ops, SparseCore 0:
  10.9 40.3 all-gather.12
  53.4 37.5 all-gather.14
  92.5 37.5 all-gather.16
  132.1 37.5 all-gather.18
  171.6 37.5 all-gather.20
  210.6 37.5 all-gather.22
